TPU v7x, 128 devices: a whole 4x4x4 slice. The times are simulated.
128 devices in a mesh: dp: 16 (over x, y_hi, core), tensor: 8 (over y_lo, z).
Axes of the slice: x: 4, y: 4 (y_hi: 2, y_lo: 2; y = y_hi * 2 + y_lo), z: 4, core: 2. Of those that a mesh axis runs over, the one named last changes fastest.
Arguments:
- grad_out: bfloat16 [4096, 4096], P('dp'), may hold values from -6 to 6
- down_weight: bfloat16 [14336, 4096], P('tensor'), may hold values from -0.046875 to 0.046875
- gate_pre: bfloat16 [4096, 14336], P('dp', 'tensor'), may hold values from -8 to 8
- up_pre: bfloat16 [4096, 14336], P('dp', 'tensor'), may hold values from -6 to 6
Outputs:
- factor: float32 [14336, 14336], P('dp', 'tensor')
- grad_up: bfloat16 [4096, 14336], P('dp', 'tensor')
All inputs are finite; a program needn't handle non-finite values.
Results may differ from a plain program's by a relative error of at most 0.0046.
Values may be sent and summed in bfloat16 or wider, within the bound.
A program may use at most 128 MiB of HBM per device.

v0:
```python
import jax
import jax.numpy as jnp
from jax import lax
from jax.sharding import PartitionSpec as P


def local(grad_out, down_weight, gate_pre, up_pre):
    hidden_grad = lax.dot_general(
        grad_out, down_weight, (((1,), (1,)), ((), ())), preferred_element_type=jnp.float32
    )
    gate_value = gate_pre.astype(jnp.float32)
    sigmoid_gate = jax.nn.sigmoid(gate_value)
    silu_slope = sigmoid_gate * (1.0 + gate_value * (1.0 - sigmoid_gate))
    grad_gate = (hidden_grad * up_pre.astype(jnp.float32) * silu_slope).astype(jnp.bfloat16)
    grad_up = (hidden_grad * gate_value * sigmoid_gate).astype(jnp.bfloat16)
    replicas = lax.axis_size("dp")
    token_total = grad_gate.shape[0] * replicas
    all_columns_grad = lax.all_gather(grad_gate, "tensor", axis=1, tiled=True)
    row_block = lax.all_to_all(all_columns_grad, "dp", split_axis=1, concat_axis=0, tiled=True)
    factor_tile = lax.dot_general(
        row_block,
        lax.all_gather(grad_gate, "dp", axis=0, tiled=True),
        (((0,), (0,)), ((), ())),
        preferred_element_type=jnp.float32,
    )
    factor = factor_tile / jnp.float32(token_total)
    return (factor, grad_up)


def solution(mesh):
    placed = (P("dp", None), P("tensor", None), P("dp", "tensor"), P("dp", "tensor"))
    return jax.shard_map(
        local,
        mesh=mesh,
        in_specs=placed,
        out_specs=(P("dp", "tensor"), P("dp", "tensor")),
        check_vma=False,
    )
```

profile of v0, /device:TPU:1, one launch (start us, length us, event | category | flops | bytes accessed | tf_op | source)
XLA Modules:
  0.0 300.6 jit_solution(8699860491449621149)
XLA Ops:
  7.2 0.0 copy-start
  7.2 0.0 all-gather.3.cloned.1.call-start
  7.2 1.5 copy-done
  8.8 16.6 %fusion.8 = (bf16[256,1792]{1,0:T(8,128)(2,1)}, bf16[256,1792]{1,0:T(8,128)(2,1)}) fusion(bf16[256,1792]{1,0:T(8,128)(2,1)} %param.6, bf16[256,1792]{1,0:T(8,128)(2,1)} %param.7, bf16[256,4096]{1,0:T(8,128)(2,1)S(1)} %copy-done, bf16[1792,4096]{1,0:T(8,128)(2,1)} %param.5), kind=kOutput, calls=%fused_computation.13 | convolution fusion | flops 3764977664 | bytes 20447232 | tf_op jit(solution)/shard_map/dot_general | solution.py:8
  25.4 0.0 all-gather.3.cloned.1.call-update
  25.4 0.0 all-gather.5.cloned.1.call-start
  25.4 0.7 all-gather.5.cloned.1.call-update
  26.1 84.7 %all-gather.3.cloned.1.call-done = bf16[256,14336]{1,0:T(8,128)(2,1)} async-done(((bf16[256,1792]{1,0:T(8,128)(2,1)}), bf16[256,14336]{1,0:T(8,128)(2,1)}) %all-gather.3.cloned.1.call-update) | async-done | bytes 7340048 | tf_op jit(solution)/shard_map/all_gather | solution.py:18
  110.8 4.2 %copy.9 = bf16[32,16,8,896]{3,2,0,1:T(8,128)(2,1)S(1)} copy(bf16[32,16,8,896]{3,2,1,0:T(8,128)(2,1)} %bitcast.12) | data formatting | bytes 14680064 | tf_op jit(solution)/shard_map/all_to_all | solution.py:19
  115.0 118.3 %all_to_all.19 = bf16[256,16,896]{2,0,1:T(8,128)(2,1)} all-to-all(bf16[256,16,896]{2,0,1:T(8,128)(2,1)S(1)} %bitcast.11), channel_id=1, replica_groups=mesh['dp'=16,'tensor'=8] {'dp'}, dimensions={1} | all-to-all | bytes 14680064 | tf_op jit(solution)/shard_map/all_to_all | solution.py:19
  233.3 40.5 %all-gather.5.cloned.1.call-done = bf16[4096,1792]{1,0:T(8,128)(2,1)} async-done(((bf16[256,1792]{1,0:T(8,128)(2,1)}), bf16[4096,1792]{1,0:T(8,128)(2,1)}) %all-gather.5.cloned.1.call-update) | async-done | bytes 14680080 | tf_op jit(solution)/shard_map/all_gather | solution.py:22
  273.7 20.0 %convolution_multiply_fusion = f32[896,1792]{1,0:T(8,128)} fusion(bf16[4096,896]{1,0:T(8,128)(2,1)} %bitcast.13, bf16[4096,1792]{1,0:T(8,128)(2,1)} %all-gather.5.cloned.1.call-done), kind=kOutput, calls=%fused_computation.1 | convolution fusion | flops 13154942976 | bytes 28442624 | tf_op jit(solution)/shard_map/dot_general | solution.py:20
Async XLA Ops:
  7.2 1.6 copy-start
  7.2 103.6 %all-gather.3.cloned.1.call-start = ((), (), s32[]{:S(2)}) async-start(), calls=%async_computation.1 | async-start | bytes 8257536 | tf_op jit(solution)/shard_map/all_gather | solution.py:18
  25.4 248.3 %all-gather.5.cloned.1.call-start = ((), (), s32[]{:S(2)}) async-start(), calls=%async_computation.2 | async-start | bytes 15597568 | tf_op jit(solution)/shard_map/all_gather | solution.py:22
Sparse Core Ops, SparseCore 0:
  25.5 85.2 all-gather.2
  113.8 159.8 all-gather.4
where the time goes:
time: 301 us
  waiting for transfers between devices  126 us (42%)
  blocking collectives  118 us (39%)
  matrix products  36.6 us (12%)
  between operations  14.1 us (5%)
  local copies, waits for them, and re-layouts  5.7 us (2%)
    all_to_all x1, blocking collectives, local(): lax.all_to_all(all_columns_grad, 'dp', split_axis=1, concat_axis=0, tiled...  118 us
    all_gather x1, waiting for transfers between devices, local(): all_columns_grad = lax.all_gather(grad_gate, 'tensor', axis=1, tiled=True)  84.7 us
    all_gather x1, waiting for transfers between devices, local(): lax.all_gather(grad_gate, 'dp', axis=0, tiled=True)  40.5 us
    dot_general x1, matrix products, local(): lax.dot_general(row_block, lax.all_gather(grad_gate, 'dp', axis=0, tiled=...  20 us
    dot_general x1, matrix products, local(): lax.dot_general(grad_out, down_weight, (((1,), (1,)), ((), ())), preferre...  16.6 us
  transfers between devices with their start and end apart: 2, of which 2 were waited for; matrix products, arithmetic and copies ran while one was open for 1% of the time, Pallas kernels for 0%

commit v1 on v0

--- a/solution.py
+++ b/solution.py
@@ -14,9 +14,19 @@
     grad_gate = (hidden_grad * up_pre.astype(jnp.float32) * silu_slope).astype(jnp.bfloat16)
     grad_up = (hidden_grad * gate_value * sigmoid_gate).astype(jnp.bfloat16)
     replicas = lax.axis_size("dp")
-    token_total = grad_gate.shape[0] * replicas
-    all_columns_grad = lax.all_gather(grad_gate, "tensor", axis=1, tiled=True)
-    row_block = lax.all_to_all(all_columns_grad, "dp", split_axis=1, concat_axis=0, tiled=True)
+    tensors = lax.axis_size("tensor")
+    tokens, hidden = grad_gate.shape
+    token_total = tokens * replicas
+    sub = tokens // tensors
+    spread = lax.all_to_all(
+        grad_gate.reshape(tensors, sub, hidden), "tensor", split_axis=0, concat_axis=0, tiled=False
+    )
+    rows = tensors * hidden // replicas
+    parts = spread.reshape(tensors, sub, hidden // rows, rows).transpose(0, 2, 1, 3)
+    parts = parts.reshape(replicas, sub, rows)
+    mine = lax.all_to_all(parts, "dp", split_axis=0, concat_axis=0, tiled=False)
+    row_block = lax.all_gather(mine, "tensor", axis=0, tiled=False)
+    row_block = row_block.transpose(1, 0, 2, 3).reshape(token_total, rows)
     factor_tile = lax.dot_general(
         row_block,
         lax.all_gather(grad_gate, "dp", axis=0, tiled=True),

time: 301 us -> 276 us (0.917)
  blocking collectives: 118 us -> 44.3 us
  waiting for transfers between devices: 126 us -> 173 us
    all_to_all x1 -> x2, blocking collectives: 118 us -> 44.3 us  [the longest x1 24.4 us: local(): mine = lax.all_to_all(parts, 'dp', split_axis=0, concat_axis=0, tiled=False)]
    all_gather x1, waiting for transfers between devices: 40.5 us -> 95.2 us  [local(): lax.all_gather(grad_gate, 'dp', axis=0, tiled=True)]
    all_gather x1, waiting for transfers between devices: 84.7 us -> 76.6 us  [local(): row_block = lax.all_gather(mine, 'tensor', axis=0, tiled=False)]
    transpose x0 -> x1, local copies, waits for them, and re-layouts: none -> 7.01 us  [local(): row_block = row_block.transpose(1, 0, 2, 3).reshape(token_total, rows)]
    all_to_all x1 -> x0, local copies, waits for them, and re-layouts: 4.16 us -> none  [local(): lax.all_to_all(all_columns_grad, 'dp', split_axis=1, concat_axis=0, tiled...]
  transfers between devices with their start and end apart: 2 -> 2, of which waited for: 2 -> 2; matrix products, arithmetic and copies ran while one was open for 1% -> 3% of each run, Pallas kernels for 0% -> 0%
where the time goes in v1:
time: 276 us
  waiting for transfers between devices  173 us (63%)
  blocking collectives  44.3 us (16%)
  matrix products  36.5 us (13%)
  between operations  14.1 us (5%)
  local copies, waits for them, and re-layouts  8.64 us (3%)
    all_gather x1, waiting for transfers between devices, local(): lax.all_gather(grad_gate, 'dp', axis=0, tiled=True)  95.2 us
    all_gather x1, waiting for transfers between devices, local(): row_block = lax.all_gather(mine, 'tensor', axis=0, tiled=False)  76.6 us
    all_to_all x1, blocking collectives, local(): mine = lax.all_to_all(parts, 'dp', split_axis=0, concat_axis=0, tiled=False)  24.4 us
    dot_general x1, matrix products, local(): lax.dot_general(row_block, lax.all_gather(grad_gate, 'dp', axis=0, tiled=...  20 us
    all_to_all x1, blocking collectives, local(): lax.all_to_all(grad_gate.reshape(tensors, sub, hidden), 'tensor', split_a...  19.8 us
    dot_general x1, matrix products, local(): lax.dot_general(grad_out, down_weight, (((1,), (1,)), ((), ())), preferre...  16.4 us
    transpose x1, local copies, waits for them, and re-layouts, local(): row_block = row_block.transpose(1, 0, 2, 3).reshape(token_total, rows)  7.01 us
  transfers between devices with their start and end apart: 2, of which 2 were waited for; matrix products, arithmetic and copies ran while one was open for 3% of the time, Pallas kernels for 0%

profile of v1, /device:TPU:1, one launch (start us, length us, event | category | flops | bytes accessed | tf_op | source)
XLA Modules:
  0.0 276.2 jit_solution(4561346166927955471)
XLA Ops:
  7.2 0.0 copy-start
  7.2 0.0 all-gather.6.cloned.1.call-start
  7.2 1.5 copy-done
  8.8 16.4 %fusion.8 = (bf16[256,1792]{1,0:T(8,128)(2,1)}, bf16[256,1792]{1,0:T(8,128)(2,1)S(1)}) fusion(bf16[256,1792]{1,0:T(8,128)(2,1)} %param.6, bf16[256,1792]{1,0:T(8,128)(2,1)} %param.7, bf16[256,4096]{1,0:T(8,128)(2,1)S(1)} %copy-done, bf16[1792,4096]{1,0:T(8,128)(2,1)} %param.5), kind=kOutput, calls=%fused_computation.12 | convolution fusion | flops 3764977664 | bytes 20447232 | tf_op jit(solution)/shard_map/dot_general | solution.py:8
  25.2 0.0 copy-start.1
  25.2 19.8 %all_to_all.10 = bf16[8,32,1792]{2,1,0:T(8,128)(2,1)S(1)} all-to-all(bf16[8,32,1792]{2,1,0:T(8,128)(2,1)S(1)} %bitcast.12), channel_id=1, replica_groups=mesh['dp'=16,'tensor'=8] {'tensor'}, dimensions={0} | all-to-all | bytes 1835008 | tf_op jit(solution)/shard_map/all_to_all | solution.py:21
  45.0 0.1 fusion.9
  45.1 0.1 pad_maximum_fusion
  45.3 0.0 copy-done.1
  45.3 24.4 %all_to_all.11 = bf16[16,32,896]{2,1,0:T(8,128)(2,1)} all-to-all(bf16[16,32,896]{2,1,0:T(8,128)(2,1)S(1)} %bitcast.13), channel_id=1, replica_groups=mesh['dp'=16,'tensor'=8] {'dp'}, dimensions={0} | all-to-all | bytes 1835008 | tf_op jit(solution)/shard_map/all_to_all | solution.py:27
  69.7 0.0 all-gather.6.cloned.1.call-update
  69.7 0.0 all-gather.4.cloned.1.call-start
  69.8 0.7 all-gather.4.cloned.1.call-update
  70.5 76.6 %all-gather.6.cloned.1.call-done = bf16[128,32,896]{2,1,0:T(8,128)(2,1)} async-done(((bf16[16,32,896]{2,1,0:T(8,128)(2,1)}), bf16[128,32,896]{2,1,0:T(8,128)(2,1)}) %all-gather.6.cloned.1.call-update) | async-done | bytes 7340048 | tf_op jit(solution)/shard_map/all_gather | solution.py:28
  147.0 7.0 %copy.7 = bf16[16,8,32,896]{3,2,1,0:T(8,128)(2,1)} copy(bf16[16,8,32,896]{3,2,0,1:T(8,128)(2,1)} %bitcast.10) | data formatting | bytes 14680064 | tf_op jit(solution)/shard_map/transpose | solution.py:29
  154.1 95.2 %all-gather.4.cloned.1.call-done = bf16[4096,1792]{1,0:T(8,128)(2,1)} async-done(((bf16[256,1792]{1,0:T(8,128)(2,1)}), bf16[4096,1792]{1,0:T(8,128)(2,1)}) %all-gather.4.cloned.1.call-update) | async-done | bytes 14680080 | tf_op jit(solution)/shard_map/all_gather | solution.py:32
  249.3 20.0 %convolution_multiply_fusion = f32[896,1792]{1,0:T(8,128)} fusion(bf16[4096,896]{1,0:T(8,128)(2,1)} %bitcast.11, bf16[4096,1792]{1,0:T(8,128)(2,1)} %all-gather.4.cloned.1.call-done), kind=kOutput, calls=%fused_computation | convolution fusion | flops 13154942976 | bytes 28442624 | tf_op jit(solution)/shard_map/dot_general | solution.py:30
Async XLA Ops:
  7.2 1.6 copy-start
  7.2 139.9 %all-gather.6.cloned.1.call-start = ((), (), s32[]{:S(2)}) async-start(), calls=%async_computation.3 | async-start | bytes 8257536 | tf_op jit(solution)/shard_map/all_gather | solution.py:28
  25.2 20.1 %copy-start.1 = (bf16[256,1792]{1,0:T(8,128)(2,1)}, bf16[256,1792]{1,0:T(8,128)(2,1)S(1)}, u32[]{:S(2)}) copy-start(bf16[256,1792]{1,0:T(8,128)(2,1)S(1)} %get-tuple-element.3) | copy-start | bytes 2752516
  69.7 179.6 %all-gather.4.cloned.1.call-start = ((), (), s32[]{:S(2)}) async-start(), calls=%async_computation.2 | async-start | bytes 15597568 | tf_op jit(solution)/shard_map/all_gather | solution.py:32
Sparse Core Ops, SparseCore 0:
  69.9 77.1 all-gather.5
  150.0 99.2 all-gather.3

commit v2 on v0

v2 whole, which is shorter than its diff:
```python
import functools

import jax
import jax.numpy as jnp
from jax import lax
from jax.experimental import pallas as pl
from jax.experimental.pallas import tpu as pltpu
from jax.sharding import PartitionSpec as P

MESH = pl.DeviceIdType.MESH
NX, NZ = 4, 4
DP, TN = 16, 8
PLANE = ((0, 2), (1, 2), (0, 1), (0, 3), (1, 1), (1, 3), (1, 0))
ARRIVE = ((1, 0), (0, 1), (0, 3), (1, 1), (1, 3), (0, 2), (1, 2))


def exchange_kernel(b_ref, out_ref, s1, rall, col, row_t, send, loc, r1, r2, colr, colp, rr):
    tokens, hidden = b_ref.shape
    sub = tokens // TN
    rows = hidden // 2
    half_tok = tokens // 2
    dp = lax.axis_index("dp")
    tn = lax.axis_index("tensor")
    x, yh, c = lax.div(dp, 4), lax.rem(lax.div(dp, 2), 2), lax.rem(dp, 2)
    yl, z = lax.div(tn, NZ), lax.rem(tn, NZ)

    def dp_of(xi, yi, ci):
        return xi * 4 + yi * 2 + ci

    def tn_of(dy, dz):
        return lax.rem(yl + dy, 2) * NZ + lax.rem(z + dz, NZ)

    x1, x3, x2 = lax.rem(x + 1, NX), lax.rem(x + 3, NX), lax.rem(x + 2, NX)
    oy = 1 - yh
    xp, xm = dp_of(x1, yh, c), dp_of(x3, yh, c)
    yc, peer = dp_of(x, oy, c), dp_of(x, yh, 1 - c)
    zp, zm, yn = tn_of(0, 1), tn_of(0, 3), tn_of(1, 0)

    barrier = pltpu.get_barrier_semaphore()
    for dy, dz in PLANE:
        pl.semaphore_signal(barrier, inc=1, device_id=(dp, tn_of(dy, dz)), device_id_type=MESH)
    for k in range(1, DP):
        pl.semaphore_signal(barrier, inc=1, device_id=(lax.rem(dp + k, DP), tn), device_id_type=MESH)
    pl.semaphore_wait(barrier, len(PLANE) + DP - 1)

    started = []

    def push(src, dst, sem, where):
        copy = pltpu.make_async_remote_copy(
            src_ref=src,
            dst_ref=dst,
            send_sem=send.at[len(started)],
            recv_sem=sem,
            device_id=where,
            device_id_type=MESH,
        )
        copy.start()
        started.append(copy)

    def arrived(ref, sem):
        pltpu.make_async_copy(ref, ref, sem).wait()

    def tok(h):
        return pl.ds(h * half_tok, half_tok)

    def col_push(slot, h, where):
        push(col.at[slot, tok(h)], col.at[slot, tok(h)], colr.at[slot, h], (where, tn))

    def col_wait(slot, h):
        arrived(col.at[slot, tok(h)], colr.at[slot, h])

    def to_peer(slot):
        push(col.at[slot], col.at[slot], colp.at[lax.div(slot, 2)], (peer, tn))

    def seg(g):
        return pl.ds(g * (DP // 2), DP // 2)

    def row_push(p, g, where):
        push(rall.at[p, seg(g)], rall.at[p, seg(g)], rr.at[p, g], (dp, where))

    def row_wait(p, g):
        arrived(rall.at[p, seg(g)], rr.at[p, g])

    for dy, dz in PLANE:
        p = tn_of(dy, dz)
        push(b_ref.at[pl.ds(pl.multiple_of(p * sub, sub), sub)], s1.at[tn], r1.at[tn], (dp, p))
    own = pltpu.make_async_copy(b_ref, col.at[dp], loc.at[0])
    own.start()
    keep = pltpu.make_async_copy(
        b_ref.at[pl.ds(pl.multiple_of(tn * sub, sub), sub)], s1.at[tn], loc.at[1]
    )
    keep.start()

    def own_push(h, where):
        push(b_ref.at[tok(h)], col.at[dp, tok(h)], colr.at[dp, h], (where, tn))

    own_push(0, xp)
    own_push(1, xm)
    own_push(0, yc)
    own_push(1, yc)
    push(b_ref, col.at[dp], colp.at[lax.div(dp, 2)], (peer, tn))

    for n, (dy, dz) in enumerate(((0, 0),) + ARRIVE):
        t = tn_of(dy, dz)
        if n == 0:
            keep.wait()
        else:
            arrived(s1.at[t], r1.at[t])
        for h in range(2):
            owner = 2 * t + h
            src = s1.at[t, :, pl.ds(h * rows, rows)]
            dst = rall.at[tn, dp]
            remote = pltpu.make_async_remote_copy(
                src_ref=src,
                dst_ref=dst,
                send_sem=send.at[len(started)],
                recv_sem=r2.at[dp],
                device_id=(owner, tn),
                device_id_type=MESH,
            )
            local = pltpu.make_async_copy(src, dst, r2.at[dp])

            @pl.when(owner != dp)
            def _():
                remote.start()

            @pl.when(owner == dp)
            def _():
                local.start()

            started.append((remote, owner))

    own_push(1, xp)
    own_push(0, xm)

    a, b = dp_of(x3, yh, c), dp_of(x1, yh, c)
    col_wait(a, 0)
    col_push(a, 0, xp)
    col_wait(b, 1)
    col_push(b, 1, xm)

    for s in range(DP):
        arrived(rall.at[tn, s], r2.at[s])
    row_push(tn, 0, zp)
    row_push(tn, 1, zm)
    row_push(tn, 0, yn)
    row_push(tn, 1, yn)
    row_push(tn, 1, zp)
    row_push(tn, 0, zm)

    col_wait(yc, 0)
    col_wait(yc, 1)
    col_push(yc, 0, xp)
    col_push(yc, 1, xm)
    col_push(yc, 1, xp)
    col_push(yc, 0, xm)
    to_peer(yc)
    col_wait(a, 1)
    to_peer(a)
    col_wait(b, 0)
    to_peer(b)
    opp = dp_of(x2, yh, c)
    col_wait(opp, 0)
    col_wait(opp, 1)
    to_peer(opp)

    row_wait(zm, 0)
    row_push(zm, 0, zp)
    row_wait(zp, 1)
    row_push(zp, 1, zm)
    row_wait(yn, 0)
    row_wait(yn, 1)
    row_push(yn, 0, zp)
    row_push(yn, 1, zm)
    row_push(yn, 1, zp)
    row_push(yn, 0, zm)

    ca, cb = dp_of(x3, oy, c), dp_of(x1, oy, c)
    col_wait(ca, 0)
    col_push(ca, 0, xp)
    col_wait(cb, 1)
    col_push(cb, 1, xm)
    col_wait(ca, 1)
    to_peer(ca)
    col_wait(cb, 0)
    to_peer(cb)
    copp = dp_of(x2, oy, c)
    col_wait(copp, 0)
    col_wait(copp, 1)
    to_peer(copp)

    yzp, yzm, zo, yzo = tn_of(1, 1), tn_of(1, 3), tn_of(0, 2), tn_of(1, 2)
    own.wait()
    for k in range(DP // 2):
        slot = 2 * k + (1 - c)
        arrived(col.at[slot], colp.at[k])

    scale = 1.0 / (DP * tokens)

    def multiply(p, first):
        row_t[...] = rall[p].reshape(DP * sub, rows).T
        start = pl.multiple_of(p * sub, sub)

        @pl.loop(0, hidden // 256)
        def _(n):
            cols = pl.ds(pl.multiple_of(n * 256, 256), 256)
            rhs = col[:, pl.ds(start, sub), cols].reshape(DP * sub, 256)
            part = jnp.dot(row_t[...], rhs, preferred_element_type=jnp.float32) * scale
            if first:
                out_ref[:, cols] = part
            else:
                out_ref[:, cols] += part

    multiply(tn, True)
    row_wait(yzm, 0)
    row_push(yzm, 0, zp)
    row_wait(yzp, 1)
    row_push(yzp, 1, zm)
    row_wait(zp, 0)
    multiply(zp, False)
    row_wait(zm, 1)
    multiply(zm, False)
    multiply(yn, False)
    row_wait(zo, 0)
    row_wait(zo, 1)
    multiply(zo, False)
    row_wait(yzp, 0)
    multiply(yzp, False)
    row_wait(yzm, 1)
    multiply(yzm, False)
    row_wait(yzo, 0)
    row_wait(yzo, 1)
    multiply(yzo, False)

    for item in started:
        if isinstance(item, tuple):
            remote, owner = item

            @pl.when(owner != dp)
            def _():
                remote.wait_send()
        else:
            item.wait_send()


def exchange(grad_gate):
    tokens, hidden = grad_gate.shape
    sub, rows = tokens // TN, hidden // 2
    return pl.pallas_call(
        exchange_kernel,
        out_shape=jax.ShapeDtypeStruct((rows, hidden), jnp.float32),
        in_specs=[pl.BlockSpec(memory_space=pltpu.VMEM)],
        out_specs=pl.BlockSpec(memory_space=pltpu.VMEM),
        scratch_shapes=[
            pltpu.VMEM((TN, sub, hidden), jnp.bfloat16),
            pltpu.VMEM((TN, DP, sub, rows), jnp.bfloat16),
            pltpu.VMEM((DP, tokens, hidden), jnp.bfloat16),
            pltpu.VMEM((rows, DP * sub), jnp.bfloat16),
            pltpu.SemaphoreType.DMA((64,)),
            pltpu.SemaphoreType.DMA((2,)),
            pltpu.SemaphoreType.DMA((TN,)),
            pltpu.SemaphoreType.DMA((DP,)),
            pltpu.SemaphoreType.DMA((DP, 2)),
            pltpu.SemaphoreType.DMA((DP // 2,)),
            pltpu.SemaphoreType.DMA((TN, 2)),
        ],
        compiler_params=pltpu.CompilerParams(
            collective_id=0, has_side_effects=True, vmem_limit_bytes=58 * 1024 * 1024
        ),
        name="exchange",
    )(grad_gate)


def local(grad_out, down_weight, gate_pre, up_pre):
    hidden_grad = lax.dot_general(
        grad_out, down_weight, (((1,), (1,)), ((), ())), preferred_element_type=jnp.float32
    )
    gate_value = gate_pre.astype(jnp.float32)
    sigmoid_gate = jax.nn.sigmoid(gate_value)
    silu_slope = sigmoid_gate * (1.0 + gate_value * (1.0 - sigmoid_gate))
    grad_gate = (hidden_grad * up_pre.astype(jnp.float32) * silu_slope).astype(jnp.bfloat16)
    grad_up = (hidden_grad * gate_value * sigmoid_gate).astype(jnp.bfloat16)
    factor = exchange(grad_gate)
    return (factor, grad_up)


def solution(mesh):
    placed = (P("dp", None), P("tensor", None), P("dp", "tensor"), P("dp", "tensor"))
    return jax.shard_map(
        local,
        mesh=mesh,
        in_specs=placed,
        out_specs=(P("dp", "tensor"), P("dp", "tensor")),
        check_vma=False,
    )
```

time: 301 us -> 145 us (0.48)
  waiting for transfers between devices: 126 us -> 0 us
  Pallas kernels: 0 us -> 120 us
  blocking collectives: 118 us -> 0 us
  matrix products: 36.6 us -> 16.6 us
  between operations: 14.1 us -> 0.65 us
    all_gather x2 -> x0, waiting for transfers between devices: 125 us -> none  [the longest x1 84.7 us: local(): all_columns_grad = lax.all_gather(grad_gate, 'tensor', axis=1, tiled=True)]
    pallas_call x0 -> x1, Pallas kernels: none -> 120 us  [exchange(): pl.pallas_call(exchange_kernel, out_shape=jax.ShapeDtypeStruct((rows, hid...]
    all_to_all x1 -> x0, blocking collectives: 118 us -> none  [local(): lax.all_to_all(all_columns_grad, 'dp', split_axis=1, concat_axis=0, tiled...]
    dot_general x1 -> x0, matrix products: 20 us -> none  [local(): lax.dot_general(row_block, lax.all_gather(grad_gate, 'dp', axis=0, tiled=...]
    unnamed x2 -> x3, local copies, waits for them, and re-layouts: 1.54 us -> 7.57 us
    all_to_all x1 -> x0, local copies, waits for them, and re-layouts: 4.16 us -> none  [local(): lax.all_to_all(all_columns_grad, 'dp', split_axis=1, concat_axis=0, tiled...]
  transfers between devices with their start and end apart: 2 -> 0, of which waited for: 2 -> 0; matrix products, arithmetic and copies ran while one was open for 1% -> 0% of each run, Pallas kernels for 0% -> 0%
where the time goes in v2:
time: 145 us; the launch traced here: 144 us
  Pallas kernels  120 us (83%)
  matrix products  16.6 us (11%)
  local copies, waits for them, and re-layouts  7.57 us (5%)
    pallas_call x1, Pallas kernels, exchange(): pl.pallas_call(exchange_kernel, out_shape=jax.ShapeDtypeStruct((rows, hid...  120 us
    dot_general x1, matrix products, local(): lax.dot_general(grad_out, down_weight, (((1,), (1,)), ((), ())), preferre...  16.6 us
    unnamed x3, local copies, waits for them, and re-layouts  7.57 us

profile of v2, /device:TPU:1, one launch (start us, length us, event | category | flops | bytes accessed | tf_op | source)
XLA Modules:
  0.0 144.4 jit_solution(4547451995191179932)
XLA Ops:
  0.6 0.0 copy-start
  0.6 1.6 %copy-done = bf16[256,4096]{1,0:T(8,128)(2,1)S(1)} copy-done((bf16[256,4096]{1,0:T(8,128)(2,1)S(1)}, bf16[256,4096]{1,0:T(8,128)(2,1)}, u32[]{:S(2)}) %copy-start) | copy-done | bytes 2097176
  2.2 16.6 %fusion.8 = (bf16[256,1792]{1,0:T(8,128)(2,1)}, bf16[256,1792]{1,0:T(8,128)(2,1)}) fusion(bf16[256,1792]{1,0:T(8,128)(2,1)} %param.6, bf16[256,1792]{1,0:T(8,128)(2,1)} %param.7, bf16[256,4096]{1,0:T(8,128)(2,1)S(1)} %copy-done, bf16[1792,4096]{1,0:T(8,128)(2,1)} %param.5), kind=kOutput, calls=%fused_computation.11 | convolution fusion | flops 3764977664 | bytes 20447232 | tf_op jit(solution)/shard_map/dot_general | solution.py:275
  18.8 119.6 %exchange.1 = f32[896,1792]{1,0:T(8,128)} custom-call(bf16[256,1792]{1,0:T(8,128)(2,1)} %get-tuple-element.3.b_ref), custom_call_target="tpu_custom_call" | custom-call | tf_op jit(solution)/shard_map/exchange/pallas_call | solution.py:249
  138.4 6.0 %copy.7 = f32[896,1792]{1,0:T(8,128)} copy(f32[896,1792]{1,0:T(8,128)} %exchange.1) | data formatting | bytes 12845056
Async XLA Ops:
  0.6 1.6 %copy-start = (bf16[256,4096]{1,0:T(8,128)(2,1)S(1)}, bf16[256,4096]{1,0:T(8,128)(2,1)}, u32[]{:S(2)}) copy-start(bf16[256,4096]{1,0:T(8,128)(2,1)} %param.4) | copy-start | bytes 6291460

commit v3 on v0

v3 whole, which is shorter than its diff:
```python
import jax
import jax.numpy as jnp
from jax import lax
from jax.experimental import pallas as pl
from jax.experimental.pallas import tpu as pltpu
from jax.sharding import PartitionSpec as P

MESH = pl.DeviceIdType.MESH
NX, NZ = 4, 4
DP, TN = 16, 8
CHUNK = 256
PLANE = ((0, 2), (1, 2), (0, 1), (0, 3), (1, 1), (1, 3), (1, 0))
ARRIVE = ((1, 0), (0, 1), (0, 3), (1, 1), (1, 3), (0, 2), (1, 2))
XORDER = (0, 1, 3, 2)


def factor_kernel(
    go_hbm, w_hbm, gate_hbm, up_hbm, out_ref, gu_ref,
    go, wv, gate, up, s1, rall, col,
    lin, send, r1, r2, colr, colp, rr,
):
    tokens, hidden = gu_ref.shape
    sub = tokens // TN
    rows = hidden // 2
    half_tok = tokens // 2
    chunks = hidden // CHUNK
    width = DP * sub
    dp = lax.axis_index("dp")
    tn = lax.axis_index("tensor")
    x, yh, c = lax.div(dp, 4), lax.rem(lax.div(dp, 2), 2), lax.rem(dp, 2)
    yl, z = lax.div(tn, NZ), lax.rem(tn, NZ)

    def dp_of(dx, yi, ci):
        return lax.rem(x + dx, NX) * 4 + yi * 2 + ci

    def tn_of(dy, dz):
        return lax.rem(yl + dy, 2) * NZ + lax.rem(z + dz, NZ)

    oy = 1 - yh
    xp, xm = dp_of(1, yh, c), dp_of(3, yh, c)
    yc, peer = dp_of(0, oy, c), dp_of(0, yh, 1 - c)
    zp, zm, yn = tn_of(0, 1), tn_of(0, 3), tn_of(1, 0)

    loads = [pltpu.make_async_copy(go_hbm, go, lin.at[chunks])]
    loads.append(pltpu.make_async_copy(gate_hbm, gate, lin.at[chunks + 1]))
    loads.append(pltpu.make_async_copy(up_hbm, up, lin.at[chunks + 2]))

    def w_load(n):
        rng = pl.ds(pl.multiple_of(n * CHUNK, CHUNK), CHUNK)
        return pltpu.make_async_copy(w_hbm.at[rng], wv.at[rng], lin.at[n])

    loads[0].start()
    w_load(0).start()
    loads[1].start()
    loads[2].start()
    for n in range(1, chunks):
        w_load(n).start()

    barrier = pltpu.get_barrier_semaphore()
    for dy, dz in PLANE:
        pl.semaphore_signal(barrier, inc=1, device_id=(dp, tn_of(dy, dz)), device_id_type=MESH)
    for k in range(1, DP):
        pl.semaphore_signal(barrier, inc=1, device_id=(lax.rem(dp + k, DP), tn), device_id_type=MESH)

    started = []

    def push(src, dst, sem, where):
        copy = pltpu.make_async_remote_copy(
            src_ref=src,
            dst_ref=dst,
            send_sem=send.at[len(started)],
            recv_sem=sem,
            device_id=where,
            device_id_type=MESH,
        )
        copy.start()
        started.append(copy)

    def arrived(ref, sem):
        pltpu.make_async_copy(ref, ref, sem).wait()

    def quarter(slot, h, k):
        return col.at[slot, pl.ds(k * half_tok, half_tok), pl.ds(h * rows, rows)]

    def col_push(slot, h, k, where):
        ref = quarter(slot, h, k)
        push(ref, ref, colr.at[slot, 2 * h + k], (where, tn))

    def col_wait(slot, h, k):
        arrived(quarter(slot, h, k), colr.at[slot, 2 * h + k])

    def to_peer(slot):
        push(col.at[slot], col.at[slot], colp.at[lax.div(slot, 2)], (peer, tn))

    def from_peer(slot):
        arrived(col.at[slot], colp.at[lax.div(slot, 2)])

    def seg(p, i):
        return rall.at[p, pl.ds(lax.rem(x + XORDER[i], NX) * 4, 4)]

    def row_push(p, i, where):
        push(seg(p, i), seg(p, i), rr.at[p, i], (dp, where))

    def row_wait(p, i):
        arrived(seg(p, i), rr.at[p, i])

    def slice_of(p, h):
        return col.at[dp, pl.ds(pl.multiple_of(p * sub, sub), sub), pl.ds(h * rows, rows)]

    def scatter_plane(h):
        for dy, dz in PLANE:
            p = tn_of(dy, dz)
            push(slice_of(p, h), s1.at[h, tn], r1.at[h, tn], (dp, p))

    def scatter_rows(h):
        for n, (dy, dz) in enumerate(((0, 0),) + ARRIVE):
            t = tn_of(dy, dz)
            if n == 0:
                src = slice_of(tn, h)
            else:
                arrived(s1.at[h, t], r1.at[h, t])
                src = s1.at[h, t]
            owner = 2 * t + h
            dst = rall.at[tn, dp]
            remote = pltpu.make_async_remote_copy(
                src_ref=src,
                dst_ref=dst,
                send_sem=send.at[len(started)],
                recv_sem=r2.at[dp],
                device_id=(owner, tn),
                device_id_type=MESH,
            )
            local = pltpu.make_async_copy(src, dst, r2.at[dp])

            @pl.when(owner != dp)
            def _():
                remote.start()

            @pl.when(owner == dp)
            def _():
                local.start()

            started.append((remote, owner))

    def chunk(n):
        w_load(n).wait()
        cols = pl.ds(pl.multiple_of(n * CHUNK, CHUNK), CHUNK)
        grad = lax.dot_general(
            go[...], wv[cols, :], (((1,), (1,)), ((), ())), preferred_element_type=jnp.float32
        )
        g = gate[:, cols].astype(jnp.float32)
        s = 1.0 / (1.0 + jnp.exp(-g))
        gu_ref[:, cols] = (grad * g * s).astype(jnp.bfloat16)
        slope = s * (1.0 + g * (1.0 - s))
        col[dp, :, cols] = (grad * up[:, cols].astype(jnp.float32) * slope).astype(jnp.bfloat16)

    for load in loads:
        load.wait()
    first_half = -(-rows // CHUNK) + 1

    @pl.loop(0, first_half)
    def _(n):
        chunk(n)

    pl.semaphore_wait(barrier, len(PLANE) + DP - 1)
    scatter_plane(0)
    col_push(dp, 0, 0, xp)
    col_push(dp, 0, 1, xm)

    @pl.loop(first_half, chunks)
    def _(n):
        chunk(n)

    col_push(dp, 0, 0, yc)
    col_push(dp, 0, 1, yc)
    scatter_plane(1)
    to_peer(dp)

    scatter_rows(0)
    col_push(dp, 0, 1, xp)
    col_push(dp, 0, 0, xm)
    scatter_rows(1)
    for k in (0, 1):
        col_push(dp, 1, k, xp)
        col_push(dp, 1, 1 - k, xm)

    a, b, opp = dp_of(3, yh, c), dp_of(1, yh, c), dp_of(2, yh, c)
    ca, cb, copp = dp_of(3, oy, c), dp_of(1, oy, c), dp_of(2, oy, c)

    def x_relay(left, right, h):
        col_wait(left, h, 0)
        col_push(left, h, 0, xp)
        col_wait(right, h, 1)
        col_push(right, h, 1, xm)

    x_relay(a, b, 0)

    for i, dx in enumerate(XORDER):
        for yi in range(2):
            for ci in range(2):
                s = lax.rem(x + dx, NX) * 4 + yi * 2 + ci
                arrived(rall.at[tn, s], r2.at[s])
        row_push(tn, i, zp)
        row_push(tn, i, zm)
        row_push(tn, i, yn)
    col_push(dp, 1, 0, yc)
    col_push(dp, 1, 1, yc)

    x_relay(a, b, 1)

    def cross(h):
        for k in range(2):
            col_wait(yc, h, k)
        for k in range(2):
            col_push(yc, h, k, xp)
            col_push(yc, h, 1 - k, xm)

    cross(0)

    def z_relay(left, right, i):
        if i % 2 == 0:
            row_wait(left, i)
            row_push(left, i, zp)
        else:
            row_wait(right, i)
            row_push(right, i, zm)

    for i in range(4):
        z_relay(zm, zp, i)

    def from_y(i):
        row_wait(yn, i)
        row_push(yn, i, zp)
        row_push(yn, i, zm)

    from_y(0)
    from_y(1)
    cross(1)
    to_peer(yc)

    def complete(slot, done):
        for h in range(2):
            for k in range(2):
                if (h, k) not in done:
                    col_wait(slot, h, k)
        to_peer(slot)

    plus, minus = ((0, 0), (1, 0)), ((0, 1), (1, 1))
    complete(a, plus)
    complete(b, minus)
    complete(opp, ())

    order = [dp_of(dx, yh, ci) for dx in (0, 3, 1, 2) for ci in range(2)]
    order += [dp_of(dx, oy, ci) for dx in (0, 3, 1, 2) for ci in range(2)]
    near, mid, far = (0, 8), (8, 12), (12, 16)
    scale = 1.0 / (DP * tokens)

    def turn(p):
        @pl.loop(0, rows // 128)
        def _(m):
            lanes = pl.ds(pl.multiple_of(m * 128, 128), 128)
            tile = jnp.concatenate([rall[p, s, :, lanes] for s in order], axis=0)
            wv[lanes, pl.ds(pl.multiple_of(p * width, width), width)] = tile.T

    def multiply(ps, span, first=False):
        lo, hi = span
        k = (hi - lo) * sub

        @pl.loop(0, hidden // 256)
        def _(n):
            cols = pl.ds(pl.multiple_of(n * 256, 256), 256)
            lhs = [
                wv[0:rows, pl.ds(pl.multiple_of(p * width + lo * sub, 128), k)] for p in ps
            ]
            rhs = [
                col[s, pl.ds(pl.multiple_of(p * sub, sub), sub), cols]
                for p in ps
                for s in order[lo:hi]
            ]
            part = scale * jnp.dot(
                jnp.concatenate(lhs, axis=1),
                jnp.concatenate(rhs, axis=0),
                preferred_element_type=jnp.float32,
            )
            if first:
                out_ref[:, cols] = part
            else:
                out_ref[:, cols] += part

    yzp, yzm, zo, yzo = tn_of(1, 1), tn_of(1, 3), tn_of(0, 2), tn_of(1, 2)

    turn(tn)
    row_wait(zp, 0)
    row_wait(zp, 2)
    turn(zp)
    for slot in (dp_of(0, yh, 1 - c), dp_of(3, yh, 1 - c), dp_of(1, yh, 1 - c), dp_of(2, yh, 1 - c)):
        from_peer(slot)
    multiply((tn, zp), near, True)
    from_y(2)
    x_relay(ca, cb, 0)
    z_relay(yzm, yzp, 0)
    z_relay(yzm, yzp, 1)
    row_wait(zm, 1)
    row_wait(zm, 3)
    turn(zm)
    from_y(3)
    for i in range(4):
        row_wait(zo, i)
    turn(zo)
    multiply((zm, zo), near)
    x_relay(ca, cb, 1)
    z_relay(yzm, yzp, 2)
    z_relay(yzm, yzp, 3)
    turn(yn)
    complete(ca, plus)
    from_peer(dp_of(0, oy, 1 - c))
    from_peer(dp_of(3, oy, 1 - c))
    multiply((tn, zp, zm, zo), mid)
    row_wait(yzp, 0)
    row_wait(yzp, 2)
    turn(yzp)
    multiply((yn, yzp), near)
    complete(cb, minus)
    complete(copp, ())
    row_wait(yzm, 1)
    row_wait(yzm, 3)
    turn(yzm)
    from_peer(dp_of(1, oy, 1 - c))
    from_peer(dp_of(2, oy, 1 - c))
    multiply((tn, zp, zm, zo), far)
    for i in range(4):
        row_wait(yzo, i)
    turn(yzo)
    multiply((yzm, yzo), near)
    multiply((yn, yzp, yzm, yzo), mid)
    multiply((yn, yzp, yzm, yzo), far)

    for item in started:
        if isinstance(item, tuple):
            remote, owner = item

            @pl.when(owner != dp)
            def _():
                remote.wait_send()
        else:
            item.wait_send()


def local(grad_out, down_weight, gate_pre, up_pre):
    tokens, hidden = gate_pre.shape
    depth = grad_out.shape[1]
    sub, rows = tokens // TN, hidden // 2
    return tuple(
        pl.pallas_call(
            factor_kernel,
            out_shape=(
                pltpu.VMEM((rows, hidden), jnp.float32),
                pltpu.VMEM((tokens, hidden), jnp.bfloat16),
            ),
            in_specs=[pl.BlockSpec(memory_space=pl.ANY)] * 4,
            out_specs=(
                pl.BlockSpec(memory_space=pltpu.VMEM),
                pl.BlockSpec(memory_space=pltpu.VMEM),
            ),
            scratch_shapes=[
                pltpu.VMEM((tokens, depth), jnp.bfloat16),
                pltpu.VMEM((hidden, depth), jnp.bfloat16),
                pltpu.VMEM((tokens, hidden), jnp.bfloat16),
                pltpu.VMEM((tokens, hidden), jnp.bfloat16),
                pltpu.VMEM((2, TN, sub, rows), jnp.bfloat16),
                pltpu.VMEM((TN, DP, sub, rows), jnp.bfloat16),
                pltpu.VMEM((DP, tokens, hidden), jnp.bfloat16),
                pltpu.SemaphoreType.DMA((hidden // CHUNK + 3,)),
                pltpu.SemaphoreType.DMA((128,)),
                pltpu.SemaphoreType.DMA((2, TN)),
                pltpu.SemaphoreType.DMA((DP,)),
                pltpu.SemaphoreType.DMA((DP, 4)),
                pltpu.SemaphoreType.DMA((DP // 2,)),
                pltpu.SemaphoreType.DMA((TN, 4)),
            ],
            compiler_params=pltpu.CompilerParams(
                collective_id=0, has_side_effects=True, vmem_limit_bytes=52 * 1024 * 1024
            ),
            name="factor",
        )(grad_out, down_weight, gate_pre, up_pre)
    )


def solution(mesh):
    placed = (P("dp", None), P("tensor", None), P("dp", "tensor"), P("dp", "tensor"))
    return jax.shard_map(
        local,
        mesh=mesh,
        in_specs=placed,
        out_specs=(P("dp", "tensor"), P("dp", "tensor")),
        check_vma=False,
    )
```

time: 301 us -> 131 us (0.44)
  Pallas kernels: 0 us -> 126 us
  waiting for transfers between devices: 126 us -> 0 us
  blocking collectives: 118 us -> 0 us
  matrix products: 36.6 us -> 0 us
  between operations: 14.1 us -> 0.64 us
    pallas_call x0 -> x1, Pallas kernels: none -> 126 us  [local(): pl.pallas_call(factor_kernel, out_shape=(pltpu.VMEM((rows, hidden), jnp.f...]
    all_gather x2 -> x0, waiting for transfers between devices: 125 us -> none  [the longest x1 84.7 us: local(): all_columns_grad = lax.all_gather(grad_gate, 'tensor', axis=1, tiled=True)]
    all_to_all x1 -> x0, blocking collectives: 118 us -> none  [local(): lax.all_to_all(all_columns_grad, 'dp', split_axis=1, concat_axis=0, tiled...]
    dot_general x2 -> x0, matrix products: 36.6 us -> none  [the longest x1 20 us: local(): lax.dot_general(row_block, lax.all_gather(grad_gate, 'dp', axis=0, tiled=...]
    all_to_all x1 -> x0, local copies, waits for them, and re-layouts: 4.16 us -> none  [local(): lax.all_to_all(all_columns_grad, 'dp', split_axis=1, concat_axis=0, tiled...]
  transfers between devices with their start and end apart: 2 -> 0, of which waited for: 2 -> 0; matrix products, arithmetic and copies ran while one was open for 1% -> 0% of each run, Pallas kernels for 0% -> 0%
where the time goes in v3:
time: 131 us
  Pallas kernels  126 us (96%)
  local copies, waits for them, and re-layouts  3.67 us (3%)
    pallas_call x1, Pallas kernels, local(): pl.pallas_call(factor_kernel, out_shape=(pltpu.VMEM((rows, hidden), jnp.f...  126 us
    unnamed x2, local copies, waits for them, and re-layouts  3.67 us

profile of v3, /device:TPU:1, one launch (start us, length us, event | category | flops | bytes accessed | tf_op | source)
XLA Modules:
  0.0 130.8 jit_solution(8142641688018607158)
XLA Ops:
  0.6 126.4 %factor.1 = (f32[896,1792]{1,0:T(8,128)S(1)}, bf16[256,1792]{1,0:T(8,128)(2,1)S(1)}) custom-call(bf16[256,4096]{1,0:T(8,128)(2,1)} %go_hbm.1, bf16[1792,4096]{1,0:T(8,128)(2,1)} %w_hbm.1, bf16[256,1792]{1,0:T(8,128)(2,1)} %gate_hbm.1, bf16[256,1792]{1,0:T(8,128)(2,1)} %up_hbm.1), custom_call_target="tpu_custom_call" | custom-call | tf_op jit(solution)/shard_map/factor/pallas_call | solution.py:354
  127.1 2.7 %copy.8 = f32[896,1792]{1,0:T(8,128)} copy(f32[896,1792]{1,0:T(8,128)S(1)} %get-tuple-element.2) | data formatting | bytes 12845056
  129.8 0.9 copy.9

commit v4 on v3

--- a/solution.py
+++ b/solution.py
@@ -9,8 +9,8 @@
 NX, NZ = 4, 4
 DP, TN = 16, 8
 CHUNK = 256
+NTILE = 1792
 PLANE = ((0, 2), (1, 2), (0, 1), (0, 3), (1, 1), (1, 3), (1, 0))
-ARRIVE = ((1, 0), (0, 1), (0, 3), (1, 1), (1, 3), (0, 2), (1, 2))
 XORDER = (0, 1, 3, 2)
 
 
@@ -111,36 +111,34 @@
         for dy, dz in PLANE:
             p = tn_of(dy, dz)
             push(slice_of(p, h), s1.at[h, tn], r1.at[h, tn], (dp, p))
+        pltpu.make_async_copy(slice_of(tn, h), s1.at[h, tn], r1.at[h, tn]).start()
 
     def scatter_rows(h):
-        for n, (dy, dz) in enumerate(((0, 0),) + ARRIVE):
-            t = tn_of(dy, dz)
-            if n == 0:
-                src = slice_of(tn, h)
-            else:
+        for dx in XORDER:
+            for yb in range(2):
+                t = lax.rem(x + dx, NX) * 2 + yb
                 arrived(s1.at[h, t], r1.at[h, t])
-                src = s1.at[h, t]
-            owner = 2 * t + h
-            dst = rall.at[tn, dp]
-            remote = pltpu.make_async_remote_copy(
-                src_ref=src,
-                dst_ref=dst,
-                send_sem=send.at[len(started)],
-                recv_sem=r2.at[dp],
-                device_id=(owner, tn),
-                device_id_type=MESH,
-            )
-            local = pltpu.make_async_copy(src, dst, r2.at[dp])
-
-            @pl.when(owner != dp)
-            def _():
-                remote.start()
-
-            @pl.when(owner == dp)
-            def _():
-                local.start()
-
-            started.append((remote, owner))
+                owner = 2 * t + h
+                src, dst = s1.at[h, t], rall.at[tn, dp]
+                remote = pltpu.make_async_remote_copy(
+                    src_ref=src,
+                    dst_ref=dst,
+                    send_sem=send.at[len(started)],
+                    recv_sem=r2.at[dp],
+                    device_id=(owner, tn),
+                    device_id_type=MESH,
+                )
+                local = pltpu.make_async_copy(src, dst, r2.at[dp])
+
+                @pl.when(owner != dp)
+                def _():
+                    remote.start()
+
+                @pl.when(owner == dp)
+                def _():
+                    local.start()
+
+                started.append((remote, owner))
 
     def chunk(n):
         w_load(n).wait()
@@ -162,30 +160,9 @@
     def _(n):
         chunk(n)
 
-    pl.semaphore_wait(barrier, len(PLANE) + DP - 1)
-    scatter_plane(0)
-    col_push(dp, 0, 0, xp)
-    col_push(dp, 0, 1, xm)
-
-    @pl.loop(first_half, chunks)
-    def _(n):
-        chunk(n)
-
-    col_push(dp, 0, 0, yc)
-    col_push(dp, 0, 1, yc)
-    scatter_plane(1)
-    to_peer(dp)
-
-    scatter_rows(0)
-    col_push(dp, 0, 1, xp)
-    col_push(dp, 0, 0, xm)
-    scatter_rows(1)
-    for k in (0, 1):
-        col_push(dp, 1, k, xp)
-        col_push(dp, 1, 1 - k, xm)
-
     a, b, opp = dp_of(3, yh, c), dp_of(1, yh, c), dp_of(2, yh, c)
     ca, cb, copp = dp_of(3, oy, c), dp_of(1, oy, c), dp_of(2, oy, c)
+    yzp, yzm, zo, yzo = tn_of(1, 1), tn_of(1, 3), tn_of(0, 2), tn_of(1, 2)
 
     def x_relay(left, right, h):
         col_wait(left, h, 0)
@@ -193,20 +170,21 @@
         col_wait(right, h, 1)
         col_push(right, h, 1, xm)
 
-    x_relay(a, b, 0)
-
-    for i, dx in enumerate(XORDER):
-        for yi in range(2):
-            for ci in range(2):
-                s = lax.rem(x + dx, NX) * 4 + yi * 2 + ci
-                arrived(rall.at[tn, s], r2.at[s])
+    def gather_rows(i):
+        xs = lax.rem(x + XORDER[i], NX) * 4
+        for k in range(4):
+            arrived(rall.at[tn, xs + k], r2.at[xs + k])
         row_push(tn, i, zp)
         row_push(tn, i, zm)
-        row_push(tn, i, yn)
-    col_push(dp, 1, 0, yc)
-    col_push(dp, 1, 1, yc)
-
-    x_relay(a, b, 1)
+
+    def own_ring(h):
+        for k in (0, 1):
+            col_push(dp, h, k, xp)
+            col_push(dp, h, 1 - k, xm)
+
+    def to_cross(h):
+        col_push(dp, h, 0, yc)
+        col_push(dp, h, 1, yc)
 
     def cross(h):
         for k in range(2):
@@ -214,8 +192,6 @@
         for k in range(2):
             col_push(yc, h, k, xp)
             col_push(yc, h, 1 - k, xm)
-
-    cross(0)
 
     def z_relay(left, right, i):
         if i % 2 == 0:
@@ -225,18 +201,14 @@
             row_wait(right, i)
             row_push(right, i, zm)
 
-    for i in range(4):
-        z_relay(zm, zp, i)
-
     def from_y(i):
         row_wait(yn, i)
         row_push(yn, i, zp)
         row_push(yn, i, zm)
 
-    from_y(0)
-    from_y(1)
-    cross(1)
-    to_peer(yc)
+    def rest(p, segments):
+        for i in segments:
+            row_wait(p, i)
 
     def complete(slot, done):
         for h in range(2):
@@ -246,14 +218,15 @@
         to_peer(slot)
 
     plus, minus = ((0, 0), (1, 0)), ((0, 1), (1, 1))
-    complete(a, plus)
-    complete(b, minus)
-    complete(opp, ())
 
     order = [dp_of(dx, yh, ci) for dx in (0, 3, 1, 2) for ci in range(2)]
     order += [dp_of(dx, oy, ci) for dx in (0, 3, 1, 2) for ci in range(2)]
     near, mid, far = (0, 8), (8, 12), (12, 16)
     scale = 1.0 / (DP * tokens)
+
+    def peer_side(*dxs, yi):
+        for dx in dxs:
+            from_peer(dp_of(dx, yi, 1 - c))
 
     def turn(p):
         @pl.loop(0, rows // 128)
@@ -266,9 +239,9 @@
         lo, hi = span
         k = (hi - lo) * sub
 
-        @pl.loop(0, hidden // 256)
+        @pl.loop(0, hidden // NTILE)
         def _(n):
-            cols = pl.ds(pl.multiple_of(n * 256, 256), 256)
+            cols = pl.ds(pl.multiple_of(n * NTILE, NTILE), NTILE)
             lhs = [
                 wv[0:rows, pl.ds(pl.multiple_of(p * width + lo * sub, 128), k)] for p in ps
             ]
@@ -287,53 +260,84 @@
             else:
                 out_ref[:, cols] += part
 
-    yzp, yzm, zo, yzo = tn_of(1, 1), tn_of(1, 3), tn_of(0, 2), tn_of(1, 2)
-
+    pl.semaphore_wait(barrier, len(PLANE) + DP - 1)
+    scatter_plane(0)
+    col_push(dp, 0, 0, xp)
+    col_push(dp, 0, 1, xm)
+
+    @pl.loop(first_half, chunks)
+    def _(n):
+        chunk(n)
+
+    scatter_plane(1)
+    to_peer(dp)
+    scatter_rows(0)
+    col_push(dp, 0, 1, xp)
+    col_push(dp, 0, 0, xm)
+    scatter_rows(1)
+    own_ring(1)
+    to_cross(0)
+    x_relay(a, b, 0)
+    gather_rows(0)
+    row_push(tn, 0, yn)
+    to_cross(1)
+    gather_rows(1)
+    gather_rows(2)
+    gather_rows(3)
+    row_push(tn, 1, yn)
+    row_push(tn, 2, yn)
+    row_push(tn, 3, yn)
     turn(tn)
-    row_wait(zp, 0)
-    row_wait(zp, 2)
+    z_relay(zm, zp, 0)
+    z_relay(zm, zp, 1)
+    x_relay(a, b, 1)
+    z_relay(zm, zp, 2)
+    cross(0)
+    z_relay(zm, zp, 3)
+    complete(a, plus)
+    complete(b, minus)
+    rest(zp, (0, 2))
+    rest(zm, (1, 3))
     turn(zp)
-    for slot in (dp_of(0, yh, 1 - c), dp_of(3, yh, 1 - c), dp_of(1, yh, 1 - c), dp_of(2, yh, 1 - c)):
-        from_peer(slot)
+    turn(zm)
+    from_y(0)
+    complete(opp, ())
+    peer_side(0, 1, 2, 3, yi=yh)
     multiply((tn, zp), near, True)
-    from_y(2)
+    rest(zo, range(4))
+    turn(zo)
+    cross(1)
+    to_peer(yc)
+    multiply((zm, zo), near)
+    from_y(1)
     x_relay(ca, cb, 0)
     z_relay(yzm, yzp, 0)
+    from_y(2)
     z_relay(yzm, yzp, 1)
-    row_wait(zm, 1)
-    row_wait(zm, 3)
-    turn(zm)
     from_y(3)
-    for i in range(4):
-        row_wait(zo, i)
-    turn(zo)
-    multiply((zm, zo), near)
+    turn(yn)
     x_relay(ca, cb, 1)
+    complete(ca, plus)
+    complete(cb, minus)
+    multiply((yn,), near)
+    peer_side(0, 3, yi=oy)
     z_relay(yzm, yzp, 2)
+    multiply((tn, zp, zm, zo), mid)
+    multiply((yn,), mid)
     z_relay(yzm, yzp, 3)
-    turn(yn)
-    complete(ca, plus)
-    from_peer(dp_of(0, oy, 1 - c))
-    from_peer(dp_of(3, oy, 1 - c))
-    multiply((tn, zp, zm, zo), mid)
-    row_wait(yzp, 0)
-    row_wait(yzp, 2)
+    complete(copp, ())
+    rest(yzp, (0, 2))
+    rest(yzm, (1, 3))
     turn(yzp)
-    multiply((yn, yzp), near)
-    complete(cb, minus)
-    complete(copp, ())
-    row_wait(yzm, 1)
-    row_wait(yzm, 3)
     turn(yzm)
-    from_peer(dp_of(1, oy, 1 - c))
-    from_peer(dp_of(2, oy, 1 - c))
+    multiply((yzp, yzm), near)
+    peer_side(1, 2, yi=oy)
     multiply((tn, zp, zm, zo), far)
-    for i in range(4):
-        row_wait(yzo, i)
+    multiply((yn, yzp, yzm), far)
+    multiply((yzp, yzm), mid)
+    rest(yzo, range(4))
     turn(yzo)
-    multiply((yzm, yzo), near)
-    multiply((yn, yzp, yzm, yzo), mid)
-    multiply((yn, yzp, yzm, yzo), far)
+    multiply((yzo,), (0, 16))
 
     for item in started:
         if isinstance(item, tuple):

time: 131 us -> 107 us (0.82)
  Pallas kernels: 126 us -> 102 us
    pallas_call x1, Pallas kernels: 126 us -> 102 us  [local(): pl.pallas_call(factor_kernel, out_shape=(pltpu.VMEM((rows, hidden), jnp.f...]
where the time goes in v4:
time: 107 us; the launch traced here: 106 us
  Pallas kernels  102 us (95%)
  local copies, waits for them, and re-layouts  3.67 us (3%)
    pallas_call x1, Pallas kernels, local(): pl.pallas_call(factor_kernel, out_shape=(pltpu.VMEM((rows, hidden), jnp.f...  102 us
    unnamed x2, local copies, waits for them, and re-layouts  3.67 us

profile of v4, /device:TPU:1, one launch (start us, length us, event | category | flops | bytes accessed | tf_op | source)
XLA Modules:
  0.0 105.8 jit_solution(4139459745064126337)
XLA Ops:
  0.6 101.5 %factor.1 = (f32[896,1792]{1,0:T(8,128)S(1)}, bf16[256,1792]{1,0:T(8,128)(2,1)S(1)}) custom-call(bf16[256,4096]{1,0:T(8,128)(2,1)} %go_hbm.1, bf16[1792,4096]{1,0:T(8,128)(2,1)} %w_hbm.1, bf16[256,1792]{1,0:T(8,128)(2,1)} %gate_hbm.1, bf16[256,1792]{1,0:T(8,128)(2,1)} %up_hbm.1), custom_call_target="tpu_custom_call" | custom-call | tf_op jit(solution)/shard_map/factor/pallas_call | solution.py:358
  102.1 2.7 %copy.8 = f32[896,1792]{1,0:T(8,128)} copy(f32[896,1792]{1,0:T(8,128)S(1)} %get-tuple-element.2) | data formatting | bytes 12845056
  104.9 0.9 copy.9

commit v5 on v4

--- a/solution.py
+++ b/solution.py
@@ -294,47 +294,46 @@
     z_relay(zm, zp, 2)
     cross(0)
     z_relay(zm, zp, 3)
+    row_push(zp, 3, yn)
     complete(a, plus)
     complete(b, minus)
     rest(zp, (0, 2))
     rest(zm, (1, 3))
+    row_push(zm, 3, yn)
     turn(zp)
     turn(zm)
     from_y(0)
     complete(opp, ())
     peer_side(0, 1, 2, 3, yi=yh)
-    multiply((tn, zp), near, True)
-    rest(zo, range(4))
-    turn(zo)
     cross(1)
     to_peer(yc)
+    multiply((tn, zp), near, True)
+    from_y(1)
+    rest(zo, range(4))
+    row_push(zo, 3, yn)
+    x_relay(ca, cb, 0)
+    from_y(2)
+    z_relay(yzm, yzp, 0)
+    turn(zo)
     multiply((zm, zo), near)
-    from_y(1)
-    x_relay(ca, cb, 0)
-    z_relay(yzm, yzp, 0)
-    from_y(2)
     z_relay(yzm, yzp, 1)
-    from_y(3)
+    x_relay(ca, cb, 1)
+    row_wait(yn, 3)
     turn(yn)
-    x_relay(ca, cb, 1)
+    multiply((yn,), near)
     complete(ca, plus)
     complete(cb, minus)
-    multiply((yn,), near)
     peer_side(0, 3, yi=oy)
+    multiply((tn, zp, zm, zo, yn), mid)
     z_relay(yzm, yzp, 2)
-    multiply((tn, zp, zm, zo), mid)
-    multiply((yn,), mid)
-    z_relay(yzm, yzp, 3)
     complete(copp, ())
-    rest(yzp, (0, 2))
+    rest(yzp, (0, 2, 3))
+    turn(yzp)
     rest(yzm, (1, 3))
-    turn(yzp)
     turn(yzm)
-    multiply((yzp, yzm), near)
+    multiply((yzp, yzm), (0, 12))
     peer_side(1, 2, yi=oy)
-    multiply((tn, zp, zm, zo), far)
-    multiply((yn, yzp, yzm), far)
-    multiply((yzp, yzm), mid)
+    multiply((tn, zp, zm, zo, yn, yzp, yzm), far)
     rest(yzo, range(4))
     turn(yzo)
     multiply((yzo,), (0, 16))

time: 107 us -> 102 us (0.953)
  Pallas kernels: 102 us -> 97.3 us
    pallas_call x1, Pallas kernels: 102 us -> 97.3 us  [local(): pl.pallas_call(factor_kernel, out_shape=(pltpu.VMEM((rows, hidden), jnp.f...]
where the time goes in v5:
time: 102 us
  Pallas kernels  97.3 us (95%)
  local copies, waits for them, and re-layouts  3.67 us (4%)
    pallas_call x1, Pallas kernels, local(): pl.pallas_call(factor_kernel, out_shape=(pltpu.VMEM((rows, hidden), jnp.f...  97.3 us
    unnamed x2, local copies, waits for them, and re-layouts  3.67 us

profile of v5, /device:TPU:1, one launch (start us, length us, event | category | flops | bytes accessed | tf_op | source)
XLA Modules:
  0.0 101.6 jit_solution(15909560560909748461)
XLA Ops:
  0.6 97.3 %factor.1 = (f32[896,1792]{1,0:T(8,128)S(1)}, bf16[256,1792]{1,0:T(8,128)(2,1)S(1)}) custom-call(bf16[256,4096]{1,0:T(8,128)(2,1)} %go_hbm.1, bf16[1792,4096]{1,0:T(8,128)(2,1)} %w_hbm.1, bf16[256,1792]{1,0:T(8,128)(2,1)} %gate_hbm.1, bf16[256,1792]{1,0:T(8,128)(2,1)} %up_hbm.1), custom_call_target="tpu_custom_call" | custom-call | tf_op jit(solution)/shard_map/factor/pallas_call | solution.py:357
  98.0 2.7 %copy.8 = f32[896,1792]{1,0:T(8,128)} copy(f32[896,1792]{1,0:T(8,128)S(1)} %get-tuple-element.2) | data formatting | bytes 12845056
  100.7 0.9 copy.9

commit v6 on v5

--- a/solution.py
+++ b/solution.py
@@ -10,13 +10,14 @@
 DP, TN = 16, 8
 CHUNK = 256
 NTILE = 1792
+TILES = (512, 512, 512, 256)
 PLANE = ((0, 2), (1, 2), (0, 1), (0, 3), (1, 1), (1, 3), (1, 0))
 XORDER = (0, 1, 3, 2)
 
 
 def factor_kernel(
-    go_hbm, w_hbm, gate_hbm, up_hbm, out_ref, gu_ref,
-    go, wv, gate, up, s1, rall, col,
+    go_hbm, w_hbm, gate_hbm, up_hbm, out_ref, gu_ref, last, col,
+    go, wv, gate, up, s1, rall,
     lin, send, r1, r2, colr, colp, rr,
 ):
     tokens, hidden = gu_ref.shape
@@ -62,19 +63,19 @@
     for k in range(1, DP):
         pl.semaphore_signal(barrier, inc=1, device_id=(lax.rem(dp + k, DP), tn), device_id_type=MESH)
 
-    started = []
-
-    def push(src, dst, sem, where):
-        copy = pltpu.make_async_remote_copy(
+    PLANE_SENDS, OWNER_SENDS, COL_SENDS, ROW_SENDS, PEER_SENDS = range(5)
+    started = [0] * 5
+
+    def push(kind, src, dst, sem, where):
+        started[kind] += 1
+        pltpu.make_async_remote_copy(
             src_ref=src,
             dst_ref=dst,
-            send_sem=send.at[len(started)],
+            send_sem=send.at[kind],
             recv_sem=sem,
             device_id=where,
             device_id_type=MESH,
-        )
-        copy.start()
-        started.append(copy)
+        ).start()
 
     def arrived(ref, sem):
         pltpu.make_async_copy(ref, ref, sem).wait()
@@ -84,13 +85,13 @@
 
     def col_push(slot, h, k, where):
         ref = quarter(slot, h, k)
-        push(ref, ref, colr.at[slot, 2 * h + k], (where, tn))
+        push(COL_SENDS, ref, ref, colr.at[lax.div(slot, 2), 2 * h + k], (where, tn))
 
     def col_wait(slot, h, k):
-        arrived(quarter(slot, h, k), colr.at[slot, 2 * h + k])
+        arrived(quarter(slot, h, k), colr.at[lax.div(slot, 2), 2 * h + k])
 
     def to_peer(slot):
-        push(col.at[slot], col.at[slot], colp.at[lax.div(slot, 2)], (peer, tn))
+        push(PEER_SENDS, col.at[slot], col.at[slot], colp.at[lax.div(slot, 2)], (peer, tn))
 
     def from_peer(slot):
         arrived(col.at[slot], colp.at[lax.div(slot, 2)])
@@ -99,7 +100,7 @@
         return rall.at[p, pl.ds(lax.rem(x + XORDER[i], NX) * 4, 4)]
 
     def row_push(p, i, where):
-        push(seg(p, i), seg(p, i), rr.at[p, i], (dp, where))
+        push(ROW_SENDS, seg(p, i), seg(p, i), rr.at[p, i], (dp, where))
 
     def row_wait(p, i):
         arrived(seg(p, i), rr.at[p, i])
@@ -110,7 +111,7 @@
     def scatter_plane(h):
         for dy, dz in PLANE:
             p = tn_of(dy, dz)
-            push(slice_of(p, h), s1.at[h, tn], r1.at[h, tn], (dp, p))
+            push(PLANE_SENDS, slice_of(p, h), s1.at[h, tn], r1.at[h, tn], (dp, p))
         pltpu.make_async_copy(slice_of(tn, h), s1.at[h, tn], r1.at[h, tn]).start()
 
     def scatter_rows(h):
@@ -123,12 +124,12 @@
                 remote = pltpu.make_async_remote_copy(
                     src_ref=src,
                     dst_ref=dst,
-                    send_sem=send.at[len(started)],
-                    recv_sem=r2.at[dp],
+                    send_sem=send.at[OWNER_SENDS],
+                    recv_sem=r2.at[x],
                     device_id=(owner, tn),
                     device_id_type=MESH,
                 )
-                local = pltpu.make_async_copy(src, dst, r2.at[dp])
+                local = pltpu.make_async_copy(src, dst, r2.at[x])
 
                 @pl.when(owner != dp)
                 def _():
@@ -138,7 +139,6 @@
                 def _():
                     local.start()
 
-                started.append((remote, owner))
 
     def chunk(n):
         w_load(n).wait()
@@ -171,9 +171,7 @@
         col_push(right, h, 1, xm)
 
     def gather_rows(i):
-        xs = lax.rem(x + XORDER[i], NX) * 4
-        for k in range(4):
-            arrived(rall.at[tn, xs + k], r2.at[xs + k])
+        arrived(seg(tn, i), r2.at[lax.rem(x + XORDER[i], NX)])
         row_push(tn, i, zp)
         row_push(tn, i, zm)
 
@@ -228,12 +226,15 @@
         for dx in dxs:
             from_peer(dp_of(dx, yi, 1 - c))
 
-    def turn(p):
+    def turn(p, into=None):
         @pl.loop(0, rows // 128)
         def _(m):
             lanes = pl.ds(pl.multiple_of(m * 128, 128), 128)
             tile = jnp.concatenate([rall[p, s, :, lanes] for s in order], axis=0)
-            wv[lanes, pl.ds(pl.multiple_of(p * width, width), width)] = tile.T
+            if into is None:
+                wv[lanes, pl.ds(pl.multiple_of(p * width, width), width)] = tile.T
+            else:
+                into[lanes, :] = tile.T
 
     def multiply(ps, span, first=False):
         lo, hi = span
@@ -324,68 +325,114 @@
     complete(ca, plus)
     complete(cb, minus)
     peer_side(0, 3, yi=oy)
-    multiply((tn, zp, zm, zo, yn), mid)
+    multiply((tn, zp), mid)
     z_relay(yzm, yzp, 2)
-    complete(copp, ())
+    multiply((zm, zo, yn), mid)
     rest(yzp, (0, 2, 3))
     turn(yzp)
     rest(yzm, (1, 3))
     turn(yzm)
+    complete(copp, ())
     multiply((yzp, yzm), (0, 12))
     peer_side(1, 2, yi=oy)
     multiply((tn, zp, zm, zo, yn, yzp, yzm), far)
     rest(yzo, range(4))
-    turn(yzo)
-    multiply((yzo,), (0, 16))
-
-    for item in started:
-        if isinstance(item, tuple):
-            remote, owner = item
-
-            @pl.when(owner != dp)
-            def _():
-                remote.wait_send()
-        else:
-            item.wait_send()
+    turn(yzo, last)
+
+    each = 4
+    assert started[COL_SENDS] % each == 0 and started[ROW_SENDS] % each == 0
+    arrived(rall.at[0, 0 : started[PLANE_SENDS]], send.at[PLANE_SENDS])
+    arrived(rall.at[0, 0 : DP - 1], send.at[OWNER_SENDS])
+    arrived(rall.at[0 : started[COL_SENDS] // each], send.at[COL_SENDS])
+    arrived(rall.at[0 : started[ROW_SENDS] // each], send.at[ROW_SENDS])
+    arrived(col.at[0 : started[PEER_SENDS]], send.at[PEER_SENDS])
+
+
+def finish_kernel(acc, gu_ref, last, col, out_hbm, gu_hbm, tiles, sem):
+    rows, hidden = acc.shape
+    tokens = gu_ref.shape[0]
+    sub = tokens // TN
+    dp = lax.axis_index("dp")
+    tn = lax.axis_index("tensor")
+    x, yh = lax.div(dp, 4), lax.rem(lax.div(dp, 2), 2)
+    p = lax.rem(lax.div(tn, NZ) + 1, 2) * NZ + lax.rem(lax.rem(tn, NZ) + 2, NZ)
+    order = [
+        lax.rem(x + dx, NX) * 4 + yi * 2 + ci
+        for yi in (yh, 1 - yh)
+        for dx in (0, 3, 1, 2)
+        for ci in range(2)
+    ]
+    copies = [pltpu.make_async_copy(gu_ref, gu_hbm, sem.at[len(TILES)])]
+    copies[0].start()
+    first = 0
+    for n, size in enumerate(TILES):
+        cols = pl.ds(first, size)
+        rhs = [col[s, pl.ds(pl.multiple_of(p * sub, sub), sub), cols] for s in order]
+        tiles[:, cols] = acc[:, cols] + (1.0 / (DP * tokens)) * jnp.dot(
+            last[...],
+            jnp.concatenate(rhs, axis=0),
+            preferred_element_type=jnp.float32,
+        )
+        copy = pltpu.make_async_copy(tiles.at[:, cols], out_hbm.at[:, cols], sem.at[n])
+        copy.start()
+        copies.append(copy)
+        first += size
+    for copy in copies:
+        copy.wait()
 
 
 def local(grad_out, down_weight, gate_pre, up_pre):
     tokens, hidden = gate_pre.shape
     depth = grad_out.shape[1]
     sub, rows = tokens // TN, hidden // 2
+    vmem = pl.BlockSpec(memory_space=pltpu.VMEM)
+    anywhere = pl.BlockSpec(memory_space=pl.ANY)
+    held = pl.pallas_call(
+        factor_kernel,
+        out_shape=(
+            pltpu.VMEM((rows, hidden), jnp.float32),
+            pltpu.VMEM((tokens, hidden), jnp.bfloat16),
+            pltpu.VMEM((rows, DP * sub), jnp.bfloat16),
+            pltpu.VMEM((DP, tokens, hidden), jnp.bfloat16),
+        ),
+        in_specs=[anywhere] * 4,
+        out_specs=(vmem,) * 4,
+        scratch_shapes=[
+            pltpu.VMEM((tokens, depth), jnp.bfloat16),
+            pltpu.VMEM((hidden, depth), jnp.bfloat16),
+            pltpu.VMEM((tokens, hidden), jnp.bfloat16),
+            pltpu.VMEM((tokens, hidden), jnp.bfloat16),
+            pltpu.VMEM((2, TN, sub, rows), jnp.bfloat16),
+            pltpu.VMEM((TN, DP, sub, rows), jnp.bfloat16),
+            pltpu.SemaphoreType.DMA((hidden // CHUNK + 3,)),
+            pltpu.SemaphoreType.DMA((5,)),
+            pltpu.SemaphoreType.DMA((2, TN)),
+            pltpu.SemaphoreType.DMA((NX,)),
+            pltpu.SemaphoreType.DMA((DP // 2, 4)),
+            pltpu.SemaphoreType.DMA((DP // 2,)),
+            pltpu.SemaphoreType.DMA((TN, 4)),
+        ],
+        compiler_params=pltpu.CompilerParams(
+            collective_id=0, has_side_effects=True, vmem_limit_bytes=34 * 1024 * 1024
+        ),
+        name="factor",
+    )(grad_out, down_weight, gate_pre, up_pre)
     return tuple(
         pl.pallas_call(
-            factor_kernel,
+            finish_kernel,
             out_shape=(
+                jax.ShapeDtypeStruct((rows, hidden), jnp.float32),
+                jax.ShapeDtypeStruct((tokens, hidden), jnp.bfloat16),
+            ),
+            in_specs=[vmem] * 4,
+            out_specs=(anywhere,) * 2,
+            scratch_shapes=[
                 pltpu.VMEM((rows, hidden), jnp.float32),
-                pltpu.VMEM((tokens, hidden), jnp.bfloat16),
-            ),
-            in_specs=[pl.BlockSpec(memory_space=pl.ANY)] * 4,
-            out_specs=(
-                pl.BlockSpec(memory_space=pltpu.VMEM),
-                pl.BlockSpec(memory_space=pltpu.VMEM),
-            ),
-            scratch_shapes=[
-                pltpu.VMEM((tokens, depth), jnp.bfloat16),
-                pltpu.VMEM((hidden, depth), jnp.bfloat16),
-                pltpu.VMEM((tokens, hidden), jnp.bfloat16),
-                pltpu.VMEM((tokens, hidden), jnp.bfloat16),
-                pltpu.VMEM((2, TN, sub, rows), jnp.bfloat16),
-                pltpu.VMEM((TN, DP, sub, rows), jnp.bfloat16),
-                pltpu.VMEM((DP, tokens, hidden), jnp.bfloat16),
-                pltpu.SemaphoreType.DMA((hidden // CHUNK + 3,)),
-                pltpu.SemaphoreType.DMA((128,)),
-                pltpu.SemaphoreType.DMA((2, TN)),
-                pltpu.SemaphoreType.DMA((DP,)),
-                pltpu.SemaphoreType.DMA((DP, 4)),
-                pltpu.SemaphoreType.DMA((DP // 2,)),
-                pltpu.SemaphoreType.DMA((TN, 4)),
+                pltpu.SemaphoreType.DMA((len(TILES) + 1,)),
             ],
-            compiler_params=pltpu.CompilerParams(
-                collective_id=0, has_side_effects=True, vmem_limit_bytes=52 * 1024 * 1024
-            ),
-            name="factor",
-        )(grad_out, down_weight, gate_pre, up_pre)
+            compiler_params=pltpu.CompilerParams(vmem_limit_bytes=12 * 1024 * 1024),
+            name="finish",
+        )(*held)
     )
 
 

time: 102 us -> 97.5 us (0.956)
  local copies, waits for them, and re-layouts: 3.67 us -> 0 us
  Pallas kernels: 97.3 us -> 95.9 us
    pallas_call x1, Pallas kernels: 97.3 us -> 92.3 us  [local(): pl.pallas_call(factor_kernel, out_shape=(pltpu.VMEM((rows, hidden), jnp.f...]
    unnamed x2 -> x0, local copies, waits for them, and re-layouts: 3.67 us -> none
    pallas_call x0 -> x1, Pallas kernels: none -> 3.67 us  [local(): pl.pallas_call(finish_kernel, out_shape=(jax.ShapeDtypeStruct((rows, hidd...]
where the time goes in v6:
time: 97.5 us; the launch traced here: 96.7 us
  Pallas kernels  95.9 us (98%)
    pallas_call x1, Pallas kernels, local(): pl.pallas_call(factor_kernel, out_shape=(pltpu.VMEM((rows, hidden), jnp.f...  92.3 us
    pallas_call x1, Pallas kernels, local(): pl.pallas_call(finish_kernel, out_shape=(jax.ShapeDtypeStruct((rows, hidd...  3.67 us

profile of v6, /device:TPU:1, one launch (start us, length us, event | category | flops | bytes accessed | tf_op | source)
XLA Modules:
  0.0 96.7 jit_solution(3579909820042964704)
XLA Ops:
  0.6 92.3 %factor.1 = (f32[896,1792]{1,0:T(8,128)S(1)}, bf16[256,1792]{1,0:T(8,128)(2,1)S(1)}, bf16[896,512]{1,0:T(8,128)(2,1)S(1)}, bf16[16,256,1792]{2,1,0:T(8,128)(2,1)S(1)}) custom-call(bf16[256,4096]{1,0:T(8,128)(2,1)} %go_hbm.1, bf16[1792,4096]{1,0:T(8,128)(2,1)} %w_hbm.1, bf16[256,1792]{1,0:T(8,128)(2,1)} %gate_hbm.1, bf16[256,1792]{1,0:T(8,128)(2,1)} %up_hbm.1), custom_call_target="tpu_custom_call" | custom-call | tf_op jit(solution)/shard_map/factor/pallas_call | solution.py:390
  92.9 3.7 %finish.1 = (f32[896,1792]{1,0:T(8,128)}, bf16[256,1792]{1,0:T(8,128)(2,1)}) custom-call(f32[896,1792]{1,0:T(8,128)S(1)} %get-tuple-element.6.acc, bf16[256,1792]{1,0:T(8,128)(2,1)S(1)} %get-tuple-element.7.gu_ref, bf16[896,512]{1,0:T(8,128)(2,1)S(1)} %get-tuple-element.8.last, bf16[16,256,1792]{2,1,0:T(8,128)(2,1)S(1)} %get-tuple-element.9.col), custom_call_target="tpu_custom_call" | custom-call | tf_op jit(solution)/shard_map/finish/pallas_call | solution.py:421

commit v7 on v6

--- a/solution.py
+++ b/solution.py
@@ -18,7 +18,7 @@
 def factor_kernel(
     go_hbm, w_hbm, gate_hbm, up_hbm, out_ref, gu_ref, last, col,
     go, wv, gate, up, s1, rall,
-    lin, send, r1, r2, colr, colp, rr,
+    lin, send, r1, r2, colr, colp, colq, rr,
 ):
     tokens, hidden = gu_ref.shape
     sub = tokens // TN
@@ -92,6 +92,18 @@
 
     def to_peer(slot):
         push(PEER_SENDS, col.at[slot], col.at[slot], colp.at[lax.div(slot, 2)], (peer, tn))
+
+    def last_to_peer(slot):
+        for h in range(2):
+            for k in range(2):
+                col_wait(slot, h, k)
+                ref = quarter(slot, h, k)
+                push(COL_SENDS, ref, ref, colq.at[2 * h + k], (peer, tn))
+
+    def last_from_peer(slot):
+        for h in range(2):
+            for k in range(2):
+                arrived(quarter(slot, h, k), colq.at[2 * h + k])
 
     def from_peer(slot):
         arrived(col.at[slot], colp.at[lax.div(slot, 2)])
@@ -218,7 +230,8 @@
     plus, minus = ((0, 0), (1, 0)), ((0, 1), (1, 1))
 
     order = [dp_of(dx, yh, ci) for dx in (0, 3, 1, 2) for ci in range(2)]
-    order += [dp_of(dx, oy, ci) for dx in (0, 3, 1, 2) for ci in range(2)]
+    order += [dp_of(0, oy, c), dp_of(0, oy, 1 - c), dp_of(3, oy, c), dp_of(1, oy, c)]
+    order += [dp_of(3, oy, 1 - c), dp_of(1, oy, 1 - c), dp_of(2, oy, c), dp_of(2, oy, 1 - c)]
     near, mid, far = (0, 8), (8, 12), (12, 16)
     scale = 1.0 / (DP * tokens)
 
@@ -317,24 +330,25 @@
     z_relay(yzm, yzp, 0)
     turn(zo)
     multiply((zm, zo), near)
+    x_relay(ca, cb, 1)
     z_relay(yzm, yzp, 1)
-    x_relay(ca, cb, 1)
     row_wait(yn, 3)
     turn(yn)
     multiply((yn,), near)
     complete(ca, plus)
     complete(cb, minus)
-    peer_side(0, 3, yi=oy)
-    multiply((tn, zp), mid)
+    peer_side(0, yi=oy)
+    multiply((tn, zp, zm, zo, yn), mid)
     z_relay(yzm, yzp, 2)
-    multiply((zm, zo, yn), mid)
     rest(yzp, (0, 2, 3))
     turn(yzp)
+    multiply((yzp,), (0, 12))
     rest(yzm, (1, 3))
     turn(yzm)
-    complete(copp, ())
-    multiply((yzp, yzm), (0, 12))
-    peer_side(1, 2, yi=oy)
+    last_to_peer(copp)
+    multiply((yzm,), (0, 12))
+    peer_side(3, 1, yi=oy)
+    last_from_peer(dp_of(2, oy, 1 - c))
     multiply((tn, zp, zm, zo, yn, yzp, yzm), far)
     rest(yzo, range(4))
     turn(yzo, last)
@@ -354,14 +368,12 @@
     sub = tokens // TN
     dp = lax.axis_index("dp")
     tn = lax.axis_index("tensor")
-    x, yh = lax.div(dp, 4), lax.rem(lax.div(dp, 2), 2)
+    x, yh, c = lax.div(dp, 4), lax.rem(lax.div(dp, 2), 2), lax.rem(dp, 2)
     p = lax.rem(lax.div(tn, NZ) + 1, 2) * NZ + lax.rem(lax.rem(tn, NZ) + 2, NZ)
-    order = [
-        lax.rem(x + dx, NX) * 4 + yi * 2 + ci
-        for yi in (yh, 1 - yh)
-        for dx in (0, 3, 1, 2)
-        for ci in range(2)
-    ]
+    places = [(dx, yh, ci) for dx in (0, 3, 1, 2) for ci in range(2)]
+    places += [(dx, 1 - yh, ci) for dx, ci in ((0, c), (0, 1 - c), (3, c), (1, c))]
+    places += [(dx, 1 - yh, ci) for dx, ci in ((3, 1 - c), (1, 1 - c), (2, c), (2, 1 - c))]
+    order = [lax.rem(x + dx, NX) * 4 + yi * 2 + ci for dx, yi, ci in places]
     copies = [pltpu.make_async_copy(gu_ref, gu_hbm, sem.at[len(TILES)])]
     copies[0].start()
     first = 0
@@ -410,6 +422,7 @@
             pltpu.SemaphoreType.DMA((NX,)),
             pltpu.SemaphoreType.DMA((DP // 2, 4)),
             pltpu.SemaphoreType.DMA((DP // 2,)),
+            pltpu.SemaphoreType.DMA((4,)),
             pltpu.SemaphoreType.DMA((TN, 4)),
         ],
         compiler_params=pltpu.CompilerParams(

time: 97.5 us -> 96.6 us (level)
  no operation moved by 1% of the time
where the time goes in v7:
time: 96.6 us; the launch traced here: 95.8 us
  Pallas kernels  95 us (98%)
    pallas_call x1, Pallas kernels, local(): pl.pallas_call(factor_kernel, out_shape=(pltpu.VMEM((rows, hidden), jnp.f...  91.4 us
    pallas_call x1, Pallas kernels, local(): pl.pallas_call(finish_kernel, out_shape=(jax.ShapeDtypeStruct((rows, hidd...  3.68 us

profile of v7, /device:TPU:1, one launch (start us, length us, event | category | flops | bytes accessed | tf_op | source)
XLA Modules:
  0.0 95.8 jit_solution(6577849938374304824)
XLA Ops:
  0.6 91.4 %factor.1 = (f32[896,1792]{1,0:T(8,128)S(1)}, bf16[256,1792]{1,0:T(8,128)(2,1)S(1)}, bf16[896,512]{1,0:T(8,128)(2,1)S(1)}, bf16[16,256,1792]{2,1,0:T(8,128)(2,1)S(1)}) custom-call(bf16[256,4096]{1,0:T(8,128)(2,1)} %go_hbm.1, bf16[1792,4096]{1,0:T(8,128)(2,1)} %w_hbm.1, bf16[256,1792]{1,0:T(8,128)(2,1)} %gate_hbm.1, bf16[256,1792]{1,0:T(8,128)(2,1)} %up_hbm.1), custom_call_target="tpu_custom_call" | custom-call | tf_op jit(solution)/shard_map/factor/pallas_call | solution.py:402
  92.0 3.7 %finish.1 = (f32[896,1792]{1,0:T(8,128)}, bf16[256,1792]{1,0:T(8,128)(2,1)}) custom-call(f32[896,1792]{1,0:T(8,128)S(1)} %get-tuple-element.6.acc, bf16[256,1792]{1,0:T(8,128)(2,1)S(1)} %get-tuple-element.7.gu_ref, bf16[896,512]{1,0:T(8,128)(2,1)S(1)} %get-tuple-element.8.last, bf16[16,256,1792]{2,1,0:T(8,128)(2,1)S(1)} %get-tuple-element.9.col), custom_call_target="tpu_custom_call" | custom-call | tf_op jit(solution)/shard_map/finish/pallas_call | solution.py:434
